TPU v7x, 512 devices: a 8x2x16 block of a 8x8x16 slice. The times are simulated.
512 devices in a mesh: obs: 2 (over y), bt: 16 (over z), freq: 8 (over x), pol: 2 (over core).
Axes of the slice: x: 8, y: 2, z: 16, core: 2. Of those that a mesh axis runs over, the one named last changes fastest.
The devices are a block of a 8x8x16 slice.
Arguments:
- gains: float32 [64, 16, 8, 7936], P(('obs', 'bt', 'pol'), 'freq'), parts along dimension 0, may hold values from -3 to 3
- visibilities: bfloat16 [64, 16, 8, 16384], P('obs', 'freq', None, ('bt', 'pol')), parts along dimension 0, may hold values from -6 to 6
- first_station: int32 [32768], P(('obs', 'bt', 'pol')), parts along dimension 0, may hold values from 0 to 61
- second_station: int32 [32768], P(('obs', 'bt', 'pol')), parts along dimension 0, may hold values from 0 to 61, as said below
- filled_row_count: int32 [64], P(('obs', 'bt', 'pol')), parts along dimension 0, may hold values from 256 to 512
- facet_dir: int32 [64], P('obs'), parts along dimension 0, may hold values from 0 to 31, each once
Outputs:
- corrected: bfloat16 [64, 16, 8, 16384], P('obs', 'freq', None, ('bt', 'pol')), parts along dimension 0
There are 2 independent parts, one for each index of `obs`. A program takes and returns all parts, laid end to end along the dimension named above; each array names one. Nothing has to cross between parts.
Inputs may be any that keep to these rules, and one draw needn't show every extreme that they name: In every row second_station differs from first_station. `facet_dir`: each direction names exactly one facet.
All inputs are finite; a program needn't handle non-finite values.
Results may differ from a plain program's by a relative error of at most 0.001.
Values sent between devices are 32-bit elements; how exact they have to be, the bound alone decides.
A program may use at most 64 MiB of HBM per device.

v0:
```python
import jax
import jax.numpy as jnp
from jax import lax
from jax.sharding import PartitionSpec as P

ARRAY_STATIONS = 62
GAIN_SLOT_COUNT = 4


def cut_along(x, dim, size):
    lengths = x.shape
    parts = x.reshape(*lengths[:dim], size, lengths[dim] // size, *lengths[dim + 1 :])
    return jnp.moveaxis(parts, dim, 0)


def joined_along(parts, dim):
    lengths = list(parts.shape[1:])
    lengths[dim] *= parts.shape[0]
    return jnp.moveaxis(parts, 0, dim).reshape(lengths)


def one_exchange(x, axis, axes, splits, concats):
    sizes = [lax.axis_size(a) for a in axes]
    parts = cut_along(x, splits[0], sizes[0])
    parts = jnp.moveaxis(cut_along(parts, splits[1] + 1, sizes[1]), 0, 1)
    inside = parts.shape[2:]
    parts = parts.reshape(-1, *inside)
    parts = lax.all_to_all(parts, axis, split_axis=0, concat_axis=0, tiled=True)
    parts = joined_along(parts.reshape(*sizes, *inside), concats[0] + 1)
    return joined_along(parts, concats[1])


def from_behind(value, axis, steps):
    count = lax.axis_size(axis)
    leading, last = (max(0, -steps), min(count, count - steps))
    return lax.ppermute(value, axis, [(source, source + steps) for source in range(leading, last)])


def entry(values, row_at, col_at):
    return (values[..., 2 * row_at + col_at, :], values[..., 4 + 2 * row_at + col_at, :])


def apply_jones(left_matrix, data, right_matrix):
    real_parts = []
    imag_parts = []
    for out_row in (0, 1):
        for out_col in (0, 1):
            total_re = jnp.zeros_like(left_matrix[..., 0, :])
            total_im = jnp.zeros_like(left_matrix[..., 0, :])
            for middle in (0, 1):
                for column in (0, 1):
                    left_re, left_im = entry(left_matrix, out_row, middle)
                    data_re, data_im = entry(data, middle, column)
                    right_re, right_im = entry(right_matrix, out_col, column)
                    prod_re = left_re * data_re - left_im * data_im
                    prod_im = left_re * data_im + left_im * data_re
                    total_re = total_re + prod_re * right_re + prod_im * right_im
                    total_im = total_im + prod_im * right_re - prod_re * right_im
            real_parts.append(total_re)
            imag_parts.append(total_im)
    return jnp.stack(real_parts + imag_parts, axis=-2)


def expand_slots(gain_window, antenna, block_rows, slots, stations):
    facets, chans, comps, _ = gain_window.shape
    current = gain_window[..., : slots * stations].reshape(facets, chans, comps, slots, stations)
    following = gain_window[..., stations:].reshape(facets, chans, comps, slots, stations)
    paired = jnp.concatenate([current, following], axis=4)
    per_slot = block_rows // slots
    grouped = antenna.reshape(slots, per_slot)
    fraction = (jnp.arange(per_slot, dtype=jnp.int32).astype(jnp.float32) + 0.5) / per_slot
    station_ids = jnp.arange(stations, dtype=jnp.int32)
    station_mask = (station_ids[None, :, None] == grouped[:, None, :]).astype(jnp.float32)
    table = jnp.concatenate([station_mask * (1.0 - fraction), station_mask * fraction], axis=1)
    spread = jnp.einsum("fckjn,jnp->fckjp", paired, table, precision=lax.Precision.HIGHEST)
    return spread.reshape(facets, chans, comps, block_rows)


def apply_correction(
    gain_window, block_visibilities, first_station_gain, second_station_gain, filled_rows
):
    block_rows = block_visibilities.shape[3]
    left_matrix = expand_slots(
        gain_window, first_station_gain, block_rows, GAIN_SLOT_COUNT, ARRAY_STATIONS
    )
    right_matrix = expand_slots(
        gain_window, second_station_gain, block_rows, GAIN_SLOT_COUNT, ARRAY_STATIONS
    )
    product = apply_jones(left_matrix, block_visibilities.astype(jnp.float32), right_matrix)
    live_mask = jnp.arange(block_rows, dtype=jnp.int32) < filled_rows
    return jnp.where(live_mask, product, 0.0 * product).astype(jnp.bfloat16)


def relay(payload):
    sectioned = one_exchange(payload, ("bt", "pol"), ("bt", "pol"), (3, 3), (0, 0))
    bt_count = lax.axis_size("bt")
    pol_count = lax.axis_size("pol")
    dims_now = sectioned.shape
    grouped = sectioned.reshape(
        (pol_count, bt_count, dims_now[0] // (pol_count * bt_count)) + dims_now[1:]
    )
    relaid = jnp.transpose(grouped, (1, 0, 2, 3, 4, 5)).reshape(dims_now)
    return relaid


def select_facets(relaid, facet_dir):
    directions = relaid.shape[0]
    onehot = (facet_dir[:, None] == jnp.arange(directions, dtype=jnp.int32)[None, :]).astype(
        jnp.float32
    )
    return jnp.einsum("fd,dckn->fckn", onehot, relaid, precision=lax.Precision.HIGHEST)


def shards(gains, visibilities, first_station, second_station, filled_row_count, facet_dir):
    chosen = select_facets(relay(gains), facet_dir)
    first_slot = chosen[..., :ARRAY_STATIONS]
    from_next = from_behind(first_slot, ("bt", "pol"), -1)
    position = lax.axis_index(("bt", "pol"))
    is_last = position == lax.axis_size(("bt", "pol")) - 1
    own_final = chosen[..., chosen.shape[3] - ARRAY_STATIONS :]
    next_slot = jnp.where(is_last, own_final, from_next)
    gain_window = jnp.concatenate([chosen, next_slot], axis=3)
    return apply_correction(
        gain_window, visibilities, first_station, second_station, filled_row_count[0]
    )


def solution(mesh):
    return jax.shard_map(
        shards,
        mesh=mesh,
        in_specs=(
            P(("obs", "bt", "pol"), "freq", None, None),
            P("obs", "freq", None, ("bt", "pol")),
            P(("obs", "bt", "pol")),
            P(("obs", "bt", "pol")),
            P(("obs", "bt", "pol")),
            P("obs"),
        ),
        out_specs=P("obs", "freq", None, ("bt", "pol")),
        check_vma=False,
    )
```

profile of v0, /device:TPU:65, one launch (start us, length us, event | category | flops | bytes accessed | tf_op | source)
XLA Modules:
  0.0 102.1 jit_solution(8990942866533894188)
XLA Ops:
  0.0 1.5 %reshape.33 = f32[1,2,8,16,496]{4,3,2,1,0:T(8,128)S(1)} reshape(f32[1,2,8,7936]{3,2,1,0:T(8,128)} %param.6) | data formatting | bytes 1015808 | tf_op jit(solution)/shard_map/reshape | solution.py:12
  1.5 0.3 copy.170
  1.9 0.1 fusion.19
  2.0 0.8 pad_maximum_fusion.2
  2.8 0.0 copy-start
  2.8 45.3 %all-to-all-start = ((f32[32,1,2,8,248]{4,3,2,1,0:T(8,128)}), f32[32,1,2,8,248]{4,3,2,1,0:T(8,128)S(1)}, u32[]{:S(2)}, u32[]{:S(2)}) async-start(f32[32,1,2,8,248]{4,3,2,1,0:T(8,128)} %bitcast.7), calls=%async_computation | async-start | bytes 1048576 | tf_op jit(solution)/shard_map/all_to_all | solution.py:28
  48.2 0.0 copy-done
  48.2 0.0 copy-start.4
  48.2 0.3 copy_convert_fusion
  48.5 33.1 %all-to-all-done = f32[32,1,2,8,248]{4,3,2,1,0:T(8,128)S(1)} async-done(((f32[32,1,2,8,248]{4,3,2,1,0:T(8,128)}), f32[32,1,2,8,248]{4,3,2,1,0:T(8,128)S(1)}, u32[]{:S(2)}, u32[]{:S(2)}) %all-to-all-start) | async-done | bytes 507936 | tf_op jit(solution)/shard_map/all_to_all | solution.py:28
  81.6 0.0 copy-done.4
  81.6 0.7 fusion.1
  82.3 2.9 %collective-permute-start = (f32[32,2,8,62]{3,0,2,1:T(8,128)S(1)}, f32[32,2,8,62]{3,0,2,1:T(8,128)S(1)}, u32[]{:S(2)}, u32[]{:S(2)}) collective-permute-start(f32[32,2,8,62]{3,0,2,1:T(8,128)S(1)} %slice.92), channel_id=1, source_target_pairs={{1,0},{16,1},{17,16},{32,17},{33,32},{48,33},{49,48},{64,49},{65,6... | collective-permute-start | bytes 380936 | tf_op jit(solution)/shard_map/ppermute | solution.py:36
  85.2 0.0 copy-start.3
  85.3 0.0 copy-start.2
  85.3 0.7 copy-done.3
  85.9 0.0 copy-done.2
  85.9 0.7 fusion.9
  87.3 1.5 %reshape.35 = f32[32,2,8,4,62]{4,3,0,2,1:T(4,128)} reshape(f32[32,2,8,248]{3,0,2,1:T(8,128)S(1)} %fusion.1) | data formatting | bytes 1015808 | tf_op jit(solution)/shard_map/reshape | solution.py:66
  88.8 1.4 %copy.23 = f32[32,2,8,4,62]{4,0,2,1,3:T(8,128)S(1)} copy(f32[32,2,8,4,62]{4,3,0,2,1:T(4,128)} %reshape.35) | data formatting | bytes 1015808 | tf_op jit(solution)/shard_map/reshape | solution.py:66
  90.2 0.0 collective-permute-done
  90.2 0.1 slice_select_fusion
  90.3 1.1 %pad_maximum_fusion.1 = f32[32,2,8,248]{3,0,2,1:T(8,128)} fusion(f32[32,2,8,62]{3,0,2,1:T(8,128)S(1)} %slice_select_fusion, f32[32,2,8,248]{3,0,2,1:T(8,128)S(1)} %fusion.1), kind=kLoop, calls=%fused_computation.7 | loop fusion | flops 126976 | bytes 1142784 | tf_op jit(solution)/shard_map/concatenate | solution.py:122
  91.4 1.6 %reshape.36 = f32[32,2,8,4,62]{4,3,0,2,1:T(4,128)S(1)} reshape(f32[32,2,8,248]{3,0,2,1:T(8,128)} %pad_maximum_fusion.1) | data formatting | bytes 1015808 | tf_op jit(solution)/shard_map/reshape | solution.py:67
  93.0 0.0 copy-start.1
  93.0 0.1 copy.24
  93.1 0.8 copy-done.1
  93.9 1.2 %convolution_bitcast_fusion = f32[32,2,8,4,128]{4,0,2,1,3:T(8,128)S(1)} fusion(f32[32,2,8,4,62]{4,0,2,1,3:T(8,128)S(1)} %copy.24, f32[32,2,8,4,62]{4,0,2,1,3:T(8,128)S(1)} %copy.23, f32[4,62,128]{2,1,0:T(8,128)S(1)} %copy-done.1, f32[4,62,128]{2,1,0:T(8,128)S(1)} %get-tuple-element.43), kind=kOutput, calls=%fused_computation.1 | convolution fusion | flops 390387712 | bytes 2318336 | tf_op jit(solution)/shard_map/fckjn,jnp->fckjp/dot_general | solution.py:75
  95.1 0.6 copy.168
  95.7 0.7 fusion.18
  96.4 1.2 %convolution_bitcast_fusion.1 = f32[32,2,8,4,128]{4,0,2,1,3:T(8,128)S(1)} fusion(f32[32,2,8,4,62]{4,0,2,1,3:T(8,128)S(1)} %copy.24, f32[32,2,8,4,62]{4,0,2,1,3:T(8,128)S(1)} %copy.23, f32[4,62,128]{2,1,0:T(8,128)S(1)} %get-tuple-element.45, f32[4,62,128]{2,1,0:T(8,128)S(1)} %get-tuple-element.46), kind=kOutput, calls=%fused_computation.2 | convolution fusion | flops 390387712 | bytes 2318336 | tf_op jit(solution)/shard_map/fckjn,jnp->fckjp/dot_general | solution.py:75
  97.7 0.6 copy.169
  98.3 0.7 fusion.17
  99.0 0.3 add_dynamic-update-slice_fusion.3
  99.3 0.2 add_dynamic-update-slice_fusion.2
  99.5 0.3 add_dynamic-update-slice_fusion.1
  99.8 0.2 add_dynamic-update-slice_fusion
  100.0 0.2 subtract_dynamic-update-slice_fusion.3
  100.2 0.2 subtract_dynamic-update-slice_fusion.2
  100.4 0.2 subtract_dynamic-update-slice_fusion.1
  100.6 0.2 subtract_dynamic-update-slice_fusion
  100.8 0.1 fusion
  101.0 1.1 %copy.44 = bf16[32,2,8,512]{3,2,1,0:T(8,128)(2,1)} copy(bf16[32,2,8,512]{3,0,2,1:T(8,128)(2,1)S(1)} %fusion) | data formatting | bytes 1048576 | tf_op jit(solution)/shard_map/convert_element_type | solution.py:91
  (3 shorter events, 0.0 us)
Async XLA Ops:
  2.8 45.4 %copy-start = (bf16[32,2,8,512]{3,2,1,0:T(8,128)(2,1)S(1)}, bf16[32,2,8,512]{3,2,1,0:T(8,128)(2,1)}, u32[]{:S(2)}) copy-start(bf16[32,2,8,512]{3,2,1,0:T(8,128)(2,1)} %param.7) | copy-start | bytes 1572868
  2.8 78.8 %all-to-all-start = ((f32[32,1,2,8,248]{4,3,2,1,0:T(8,128)}), f32[32,1,2,8,248]{4,3,2,1,0:T(8,128)S(1)}, u32[]{:S(2)}, u32[]{:S(2)}) async-start(f32[32,1,2,8,248]{4,3,2,1,0:T(8,128)} %bitcast.7), calls=%async_computation | async-start | bytes 1048576 | tf_op jit(solution)/shard_map/all_to_all | solution.py:28
  48.2 33.4 %copy-start.4 = (s32[32]{0:T(128)S(1)}, s32[32]{0:T(128)}, u32[]{:S(2)}) copy-start(s32[32]{0:T(128)} %param.11) | copy-start | bytes 388
  82.3 7.8 %collective-permute-start = (f32[32,2,8,62]{3,0,2,1:T(8,128)S(1)}, f32[32,2,8,62]{3,0,2,1:T(8,128)S(1)}, u32[]{:S(2)}, u32[]{:S(2)}) collective-permute-start(f32[32,2,8,62]{3,0,2,1:T(8,128)S(1)} %slice.92), channel_id=1, source_target_pairs={{1,0},{16,1},{17,16},{32,17},{33,32},{48,33},{49,48},{64,49},{65,6... | collective-permute-start | bytes 380936 | tf_op jit(solution)/shard_map/ppermute | solution.py:36
  85.2 0.7 copy-start.3
  85.3 0.7 copy-start.2
  93.0 0.9 copy-start.1
where the time goes:
time: 102 us
  starting transfers between devices  48.2 us (47%)
  waiting for transfers between devices  33.1 us (32%)
  local copies, waits for them, and re-layouts  11.7 us (11%)
  other arithmetic  5 us (5%)
  matrix products  3.15 us (3%)
    all_to_all x1, starting transfers between devices, one_exchange(): parts = lax.all_to_all(parts, axis, split_axis=0, concat_axis=0, tiled=True)  45.3 us
    all_to_all x1, waiting for transfers between devices, one_exchange(): parts = lax.all_to_all(parts, axis, split_axis=0, concat_axis=0, tiled=True)  33.1 us
    ppermute x1, starting transfers between devices, from_behind(): lax.ppermute(value, axis, [(source, source + steps) for source in range(l...  2.9 us
    reshape x2, local copies, waits for them, and re-layouts, expand_slots(): gain_window[..., :slots * stations]  2.85 us
    dot_general x2, matrix products, expand_slots(): jnp.einsum('fckjn,jnp->fckjp', paired, table, precision=lax.Precision.HIG...  2.44 us
  transfers between devices with their start and end apart: 2, of which 1 were waited for; matrix products, arithmetic and copies ran while one was open for 4% of the time, Pallas kernels for 0%

commit v1 on v0

v1 whole, which is shorter than its diff:
```python
import functools

import jax
import jax.numpy as jnp
from jax import lax
from jax.experimental import pallas as pl
from jax.experimental.pallas import tpu as pltpu
from jax.sharding import PartitionSpec as P

ARRAY_STATIONS = 62
GAIN_SLOT_COUNT = 4
LANES = 128
TILES = 5
MESH = pl.DeviceIdType.MESH


def gather_lanes(tile, index):
    return jnp.take_along_axis(tile, index, axis=1, mode="promise_in_bounds")


def window(held, chan, start):
    tile, shift = divmod(start, LANES)
    here = held[chan, :, tile * LANES : (tile + 1) * LANES]
    if shift == 0:
        return here
    lane = lax.broadcasted_iota(jnp.int32, here.shape, 1)
    if (tile + 1) * LANES < held.shape[2]:
        after = held[chan, :, (tile + 1) * LANES : (tile + 2) * LANES]
        here = jnp.where(lane >= shift, here, after)
    return pltpu.roll(here, LANES - shift, 1)


def kernel(
    peers,
    bt_count,
    pol_count,
    filled_ref,
    facet_dir_ref,
    first_ref,
    second_ref,
    gains_hbm,
    vis_hbm,
    out_ref,
    held,
    outgoing,
    incoming,
    vis,
    done,
    left_rows,
    right_rows,
    data_rows,
    out_rows,
    gains_sem,
    vis_sem,
    send_sem,
    recv_sem,
):
    chans = held.shape[0]
    slots = GAIN_SLOT_COUNT
    rotate = jnp.where((lax.axis_index("obs") == 0) & (lax.axis_index("freq") == 0), 1, 0)
    me = lax.axis_index("bt") * pol_count + lax.axis_index("pol")
    rank = lax.rem(me - rotate + peers, peers)

    def place(order):
        return lax.rem(order + rotate, peers)

    def device(where):
        return {"bt": where // pol_count, "pol": lax.rem(where, pol_count)}

    def to(where):
        return pltpu.make_async_remote_copy(
            src_ref=outgoing.at[where],
            dst_ref=incoming.at[me],
            send_sem=send_sem.at[where],
            recv_sem=recv_sem.at[me],
            device_id=device(where),
            device_id_type=MESH,
        )

    def arrival(where):
        return pltpu.make_async_remote_copy(
            src_ref=outgoing.at[where],
            dst_ref=incoming.at[where],
            send_sem=send_sem.at[where],
            recv_sem=recv_sem.at[where],
            device_id=device(where),
            device_id_type=MESH,
        )

    load_gains = pltpu.make_async_copy(gains_hbm.at[0], held, gains_sem)
    load_gains.start()
    load_vis = pltpu.make_async_copy(vis_hbm, vis, vis_sem)
    load_vis.start()

    barrier = pltpu.get_barrier_semaphore()

    @pl.when(rank > 0)
    def _():
        pl.semaphore_wait(barrier, 1)

    @pl.when(rank < peers - 1)
    def _():
        pl.semaphore_signal(barrier, inc=1, device_id=device(place(rank + 1)), device_id_type=MESH)

    load_gains.wait()
    lane = lax.broadcasted_iota(jnp.int32, (8, LANES), 1)
    total_slots = peers * slots
    for where in range(peers):
        base = where * slots
        for chan in range(chans):
            for half in range(2):
                outgoing[where, chan * 2 + half] = window(held, chan, (base + 2 * half) * ARRAY_STATIONS)
        last = min(base + slots, total_slots - 1) * ARRAY_STATIONS
        outgoing[where, 2 * chans] = jnp.where(
            lane < LANES // 2, window(held, 0, last), pltpu.roll(window(held, 1, last), LANES // 2, 1)
        )
    incoming[me] = outgoing[me]

    def send_down(order, carry):
        to(place(order)).start()
        return carry

    lax.fori_loop(0, rank, send_down, 0)

    unit = lax.broadcasted_iota(jnp.int32, (8, LANES), 0)
    slot_of_unit = lax.rem(unit, slots)
    live = slot_of_unit * LANES + lane < filled_ref[0]
    after = (lane.astype(jnp.float32) + 0.5) / LANES
    before = 1.0 - after
    load_vis.wait()

    def spread(where, ref, rows):
        for slot in range(slots):
            station = jnp.broadcast_to(ref[slot : slot + 1, :], (8, LANES))
            upper = station + ARRAY_STATIONS
            for chan in range(chans):
                now = incoming[where, chan * 2 + slot // 2]
                if slot % 2 == 0:
                    low, high = gather_lanes(now, station), gather_lanes(now, upper)
                else:
                    low = gather_lanes(now, upper)
                    if slot + 1 < slots:
                        high = gather_lanes(incoming[where, chan * 2 + slot // 2 + 1], station)
                    else:
                        high = gather_lanes(incoming[where, 2 * chans], station + chan * (LANES // 2))
                at = (chan * slots + slot) * 8
                rows[at : at + 8, :] = before * low + after * high

    def component(rows, k):
        return rows[pl.ds(k, 8, stride=8), :]

    def correct(where):
        spread(where, first_ref, left_rows)
        spread(where, second_ref, right_rows)
        left = [component(left_rows, k) for k in range(8)]
        right = [component(right_rows, k) for k in range(8)]
        data = [component(data_rows, k) for k in range(8)]
        for row in (0, 1):
            half_re, half_im = [], []
            for column in (0, 1):
                re = im = None
                for middle in (0, 1):
                    l_re, l_im = left[2 * row + middle], left[4 + 2 * row + middle]
                    d_re, d_im = data[2 * middle + column], data[4 + 2 * middle + column]
                    p_re = l_re * d_re - l_im * d_im
                    p_im = l_re * d_im + l_im * d_re
                    re = p_re if re is None else re + p_re
                    im = p_im if im is None else im + p_im
                half_re.append(re)
                half_im.append(im)
            for out in (0, 1):
                re = im = None
                for column in (0, 1):
                    r_re, r_im = right[2 * out + column], right[4 + 2 * out + column]
                    p_re = half_re[column] * r_re + half_im[column] * r_im
                    p_im = half_im[column] * r_re - half_re[column] * r_im
                    re = p_re if re is None else re + p_re
                    im = p_im if im is None else im + p_im
                out_rows[pl.ds(2 * row + out, 8, stride=8), :] = jnp.where(live, re, 0.0)
                out_rows[pl.ds(4 + 2 * row + out, 8, stride=8), :] = jnp.where(live, im, 0.0)
        for chan in range(chans):
            for slot in range(slots):
                at = (chan * slots + slot) * 8
                done[where, chan, :, slot * LANES : (slot + 1) * LANES] = out_rows[at : at + 8, :].astype(done.dtype)

    def step(order, carry):
        where = place(order)
        facet = jnp.int32(0)
        for f in range(peers):
            facet = jnp.where(facet_dir_ref[f] == where, f, facet)
        for chan in range(chans):
            for slot in range(slots):
                at = (chan * slots + slot) * 8
                data_rows[at : at + 8, :] = vis[facet, chan, :, slot * LANES : (slot + 1) * LANES].astype(jnp.float32)

        @pl.when(order != rank)
        def _():
            arrival(where).wait_recv()

        @pl.when(order > rank)
        def _():
            to(where).start()

        correct(where)
        return carry

    lax.fori_loop(0, peers, step, 0)

    def finish(order, carry):
        @pl.when(order != rank)
        def _():
            to(place(order)).wait_send()

        return carry

    lax.fori_loop(0, peers, finish, 0)
    for f in range(peers):
        out_ref[f] = done[facet_dir_ref[f]]


def shards(gains, visibilities, first_station, second_station, filled_row_count, facet_dir):
    bt_count, pol_count = lax.axis_size("bt"), lax.axis_size("pol")
    peers = bt_count * pol_count
    chans = gains.shape[1]
    any_spec = pl.BlockSpec(memory_space=pl.ANY)
    smem = pl.BlockSpec(memory_space=pltpu.SMEM)
    vmem = pl.BlockSpec(memory_space=pltpu.VMEM)
    rows = 8 * chans * GAIN_SLOT_COUNT
    return pl.pallas_call(
        functools.partial(kernel, peers, bt_count, pol_count),
        name="correct",
        out_shape=jax.ShapeDtypeStruct(visibilities.shape, visibilities.dtype),
        in_specs=[smem, smem, vmem, vmem, any_spec, any_spec],
        out_specs=vmem,
        scratch_shapes=[
            pltpu.VMEM(gains.shape[1:], jnp.float32),
            pltpu.VMEM((peers, TILES, 8, LANES), jnp.float32),
            pltpu.VMEM((peers, TILES, 8, LANES), jnp.float32),
            pltpu.VMEM(visibilities.shape, visibilities.dtype),
            pltpu.VMEM(visibilities.shape, visibilities.dtype),
            pltpu.VMEM((rows, LANES), jnp.float32),
            pltpu.VMEM((rows, LANES), jnp.float32),
            pltpu.VMEM((rows, LANES), jnp.float32),
            pltpu.VMEM((rows, LANES), jnp.float32),
            pltpu.SemaphoreType.DMA,
            pltpu.SemaphoreType.DMA,
            pltpu.SemaphoreType.DMA((peers,)),
            pltpu.SemaphoreType.DMA((peers,)),
        ],
        compiler_params=pltpu.CompilerParams(collective_id=0, has_side_effects=True),
    )(
        filled_row_count,
        facet_dir,
        first_station.reshape(GAIN_SLOT_COUNT, LANES),
        second_station.reshape(GAIN_SLOT_COUNT, LANES),
        gains,
        visibilities,
    )


def solution(mesh):
    return jax.shard_map(
        shards,
        mesh=mesh,
        in_specs=(
            P(("obs", "bt", "pol"), "freq", None, None),
            P("obs", "freq", None, ("bt", "pol")),
            P(("obs", "bt", "pol")),
            P(("obs", "bt", "pol")),
            P(("obs", "bt", "pol")),
            P("obs"),
        ),
        out_specs=P("obs", "freq", None, ("bt", "pol")),
        check_vma=False,
    )
```

time: 102 us -> 85.5 us (0.84)
  the two profiles are of different devices: /device:TPU:65 before, /device:TPU:64 now
where the time goes in v1:
time: 85.5 us; the launch traced here: 85.3 us
  Pallas kernels  82.8 us (97%)
  local copies, waits for them, and re-layouts  1.87 us (2%)
    pallas_call x1, Pallas kernels, shards(): pl.pallas_call(functools.partial(kernel, peers, bt_count, pol_count), nam...  82.8 us
    unnamed x1, local copies, waits for them, and re-layouts  1.87 us

profile of v1, /device:TPU:64, one launch (start us, length us, event | category | flops | bytes accessed | tf_op | source)
XLA Modules:
  0.0 85.3 jit_solution(9844474355046378181)
XLA Ops:
  0.7 82.8 %correct.1 = bf16[32,2,8,512]{3,2,1,0:T(8,128)(2,1)} custom-call(s32[1]{0:T(128)S(6)} %copy.8.filled_ref, s32[32]{0:T(128)} %facet_dir_ref.1, s32[4,128]{1,0:T(4,128)} %bitcast.2, s32[4,128]{1,0:T(4,128)} %bitcast.3, f32[1,2,8,7936]{3,2,1,0:T(8,128)} %gains_hbm.1, bf16[32,2,8,512]{3,2,1,0:T(8,128)(2,1)} %vis_hbm.1), custom_call_target="tpu_custom_call" | custom-call | tf_op jit(solution)/shard_map/correct/pallas_call | solution.py:229
  83.4 1.9 %copy.9 = bf16[32,2,8,512]{3,2,1,0:T(8,128)(2,1)} copy(bf16[32,2,8,512]{3,2,1,0:T(8,128)(2,1)} %correct.1) | data formatting | bytes 1048576

commit v2 on v1

--- a/solution.py
+++ b/solution.py
@@ -11,6 +11,10 @@
 GAIN_SLOT_COUNT = 4
 LANES = 128
 TILES = 5
+IN_FLIGHT = 2
+URGENT_LAYERS = 2
+LATE_LAYERS = 3
+LAG = 4
 MESH = pl.DeviceIdType.MESH
 
 
@@ -35,12 +39,15 @@
     bt_count,
     pol_count,
     filled_ref,
+    facet_dir_hbm,
+    first_hbm,
+    second_hbm,
+    gains_hbm,
+    vis_hbm,
+    out_ref,
     facet_dir_ref,
     first_ref,
     second_ref,
-    gains_hbm,
-    vis_hbm,
-    out_ref,
     held,
     outgoing,
     incoming,
@@ -50,62 +57,90 @@
     right_rows,
     data_rows,
     out_rows,
-    gains_sem,
-    vis_sem,
+    load_sem,
+    urgent_sem,
     send_sem,
     recv_sem,
+    entered,
+    go,
 ):
     chans = held.shape[0]
     slots = GAIN_SLOT_COUNT
+    layers, half = peers // pol_count, bt_count // 2
     rotate = jnp.where((lax.axis_index("obs") == 0) & (lax.axis_index("freq") == 0), 1, 0)
-    me = lax.axis_index("bt") * pol_count + lax.axis_index("pol")
-    rank = lax.rem(me - rotate + peers, peers)
+    rank = lax.rem(lax.axis_index("bt") * pol_count + lax.axis_index("pol") + peers - rotate, peers)
+    layer = rank // pol_count
+    partner = layer * pol_count + lax.rem(rank + 1, pol_count)
 
     def place(order):
         return lax.rem(order + rotate, peers)
 
-    def device(where):
+    def device(order):
+        where = place(order)
         return {"bt": where // pol_count, "pol": lax.rem(where, pol_count)}
 
-    def to(where):
+    def to(order, sem):
         return pltpu.make_async_remote_copy(
-            src_ref=outgoing.at[where],
-            dst_ref=incoming.at[me],
-            send_sem=send_sem.at[where],
-            recv_sem=recv_sem.at[me],
-            device_id=device(where),
+            src_ref=outgoing.at[place(order)],
+            dst_ref=incoming.at[rank],
+            send_sem=sem,
+            recv_sem=recv_sem.at[layer],
+            device_id=device(order),
             device_id_type=MESH,
         )
 
-    def arrival(where):
+    def transfers(start, count, sem, into):
         return pltpu.make_async_remote_copy(
-            src_ref=outgoing.at[where],
-            dst_ref=incoming.at[where],
-            send_sem=send_sem.at[where],
-            recv_sem=recv_sem.at[where],
-            device_id=device(where),
+            src_ref=outgoing.at[pl.ds(start, count)],
+            dst_ref=incoming.at[pl.ds(start, count)],
+            send_sem=sem,
+            recv_sem=recv_sem.at[into],
+            device_id=device(partner),
             device_id_type=MESH,
         )
 
-    load_gains = pltpu.make_async_copy(gains_hbm.at[0], held, gains_sem)
-    load_gains.start()
-    load_vis = pltpu.make_async_copy(vis_hbm, vis, vis_sem)
-    load_vis.start()
+    def signal(sem, order):
+        pl.semaphore_signal(sem, inc=1, device_id=device(order), device_id_type=MESH)
+
+    loads = [
+        pltpu.make_async_copy(source, target, load_sem.at[i])
+        for i, (source, target) in enumerate(
+            (
+                (gains_hbm.at[0], held),
+                (first_hbm, first_ref),
+                (second_hbm, second_ref),
+                (facet_dir_hbm, facet_dir_ref),
+                (vis_hbm, vis),
+            )
+        )
+    ]
+    for load in loads:
+        load.start()
 
     barrier = pltpu.get_barrier_semaphore()
 
     @pl.when(rank > 0)
     def _():
-        pl.semaphore_wait(barrier, 1)
+        with jax.named_scope("chain"):
+            pl.semaphore_wait(barrier, 1)
 
     @pl.when(rank < peers - 1)
     def _():
-        pl.semaphore_signal(barrier, inc=1, device_id=device(place(rank + 1)), device_id_type=MESH)
-
-    load_gains.wait()
+        signal(barrier, rank + 1)
+
+    def greet(order, carry):
+        signal(entered.at[layer], order)
+        return carry
+
+    lax.fori_loop(0, rank, greet, 0)
+
+    with jax.named_scope("gains"):
+        loads[0].wait()
     lane = lax.broadcasted_iota(jnp.int32, (8, LANES), 1)
     total_slots = peers * slots
-    for where in range(peers):
+    urgent = URGENT_LAYERS * pol_count
+
+    def pack(where):
         base = where * slots
         for chan in range(chans):
             for half in range(2):
@@ -114,20 +149,87 @@
         outgoing[where, 2 * chans] = jnp.where(
             lane < LANES // 2, window(held, 0, last), pltpu.roll(window(held, 1, last), LANES // 2, 1)
         )
-    incoming[me] = outgoing[me]
-
-    def send_down(order, carry):
-        to(place(order)).start()
+
+    def send(order, carry):
+        to(order, send_sem).start()
         return carry
 
-    lax.fori_loop(0, rank, send_down, 0)
+    def hasten(order, carry):
+        to(order, urgent_sem.at[order]).start()
+        return carry
+
+    def hasten_next(order, carry):
+        to(order - IN_FLIGHT, urgent_sem.at[order - IN_FLIGHT]).wait_send()
+        return hasten(order, carry)
+
+    def hastened(order, carry):
+        to(order, urgent_sem.at[order]).wait_send()
+        return carry
+
+    hurry = jnp.minimum(rank, urgent)
+    for where in range(urgent + 1):
+        pack(where)
+    with jax.named_scope("urgent"):
+        lax.fori_loop(0, jnp.minimum(rank, IN_FLIGHT), hasten, 0)
+        for where in range(urgent + 1, peers):
+            pack(where)
+        lax.fori_loop(IN_FLIGHT, hurry, hasten_next, 0)
+        lax.fori_loop(jnp.maximum(hurry - IN_FLIGHT, 0), hurry, hastened, 0)
+
+    late = layers - LATE_LAYERS
+    far_above = jnp.where(rank < urgent, layers, jnp.minimum(jnp.maximum(layer + half, late), layers))
+    far_below = jnp.where(layer < late, URGENT_LAYERS, jnp.maximum(layer - half + 1, URGENT_LAYERS))
+
+    def send_far():
+        @pl.when((rank >= urgent) & (layer < half))
+        def _():
+            with jax.named_scope("go"):
+                pl.semaphore_wait(go, 1)
+            lax.fori_loop(far_above * pol_count, peers, send, 0)
+
+        @pl.when((layer >= late) & (layer < layers - 1))
+        def _():
+            def turn_of(low, carry):
+                with jax.named_scope("go"):
+                    pl.semaphore_wait(go, 1)
+                for core in range(pol_count):
+                    send(low * pol_count + core, 0)
+                return carry
+
+            lax.fori_loop(URGENT_LAYERS, far_below, turn_of, 0)
+
+        @pl.when(layer == layers - 1)
+        def _():
+            def turn_of(low, carry):
+                @pl.when(rank == peers - pol_count)
+                def _():
+                    for core in range(pol_count):
+                        signal(go, low * pol_count + core)
+
+                    def release(order, carry):
+                        signal(go, order)
+                        return carry
+
+                    lax.fori_loop(jnp.maximum(low + half, late) * pol_count, peers - pol_count, release, 0)
+
+                for core in range(pol_count):
+                    to(low * pol_count + core, urgent_sem.at[core]).start()
+                for core in range(pol_count):
+                    to(low * pol_count + core, urgent_sem.at[core]).wait_send()
+                return carry
+
+            lax.fori_loop(URGENT_LAYERS, far_below, turn_of, 0)
+
+    incoming[rank] = outgoing[place(rank)]
+    with jax.named_scope("loads"):
+        for load in loads[1:]:
+            load.wait()
 
     unit = lax.broadcasted_iota(jnp.int32, (8, LANES), 0)
     slot_of_unit = lax.rem(unit, slots)
     live = slot_of_unit * LANES + lane < filled_ref[0]
     after = (lane.astype(jnp.float32) + 0.5) / LANES
     before = 1.0 - after
-    load_vis.wait()
 
     def spread(where, ref, rows):
         for slot in range(slots):
@@ -149,9 +251,9 @@
     def component(rows, k):
         return rows[pl.ds(k, 8, stride=8), :]
 
-    def correct(where):
-        spread(where, first_ref, left_rows)
-        spread(where, second_ref, right_rows)
+    def correct(order, where):
+        spread(order, first_ref, left_rows)
+        spread(order, second_ref, right_rows)
         left = [component(left_rows, k) for k in range(8)]
         right = [component(right_rows, k) for k in range(8)]
         data = [component(data_rows, k) for k in range(8)]
@@ -183,7 +285,7 @@
                 at = (chan * slots + slot) * 8
                 done[where, chan, :, slot * LANES : (slot + 1) * LANES] = out_rows[at : at + 8, :].astype(done.dtype)
 
-    def step(order, carry):
+    def take(order):
         where = place(order)
         facet = jnp.int32(0)
         for f in range(peers):
@@ -192,47 +294,113 @@
             for slot in range(slots):
                 at = (chan * slots + slot) * 8
                 data_rows[at : at + 8, :] = vis[facet, chan, :, slot * LANES : (slot + 1) * LANES].astype(jnp.float32)
-
-        @pl.when(order != rank)
-        def _():
-            arrival(where).wait_recv()
-
-        @pl.when(order > rank)
-        def _():
-            to(where).start()
-
-        correct(where)
+        correct(order, where)
+
+    with jax.named_scope("own"):
+        take(rank)
+    above = layers - 1 - layer
+    near_above = far_above - 1 - layer
+
+    def answer(turn, carry):
+        @pl.when((turn == 0) & (rank < partner))
+        def _():
+            pl.semaphore_wait(entered.at[layer], pol_count - 1)
+            send(partner, 0)
+
+        @pl.when((turn == 0) & (rank > partner) & (rank >= urgent))
+        def _():
+            send(partner, 0)
+
+        @pl.when((turn > 0) & (turn <= above))
+        def _():
+            with jax.named_scope("hello"):
+                pl.semaphore_wait(entered.at[layer + turn], pol_count)
+
+            @pl.when(layer + turn < far_above)
+            def _():
+                for core in range(pol_count):
+                    send((layer + turn) * pol_count + core, 0)
+
+        first = jnp.where(turn == 0, far_below, far_below + turn + 1)
+        last = jnp.where(turn < above, jnp.minimum(far_below + turn + 2, layer), jnp.where(turn == above, layer, 0))
+
+        def send_near(low, carry):
+            for core in range(pol_count):
+                send(low * pol_count + core, 0)
+            return carry
+
+        lax.fori_loop(first, last, send_near, 0)
+
+        @pl.when(turn == above)
+        def _():
+            send_far()
+
+        step = turn - LAG
+
+        @pl.when(step == 0)
+        def _():
+            transfers(partner, pol_count - 1, send_sem, layer).wait_recv()
+            take(partner)
+
+        @pl.when(step > 0)
+        def _():
+            source = jnp.where(step <= near_above, layer + step, step)
+            source = jnp.where((step > near_above) & (step <= near_above + layer), step - near_above - 1, source)
+            with jax.named_scope("arrive"):
+                transfers(source * pol_count, pol_count, send_sem, source).wait_recv()
+            with jax.named_scope("correct"):
+
+                def both(core, carry):
+                    take(source * pol_count + core)
+                    return carry
+
+                lax.fori_loop(0, pol_count, both, 0)
+
         return carry
 
-    lax.fori_loop(0, peers, step, 0)
-
-    def finish(order, carry):
-        @pl.when(order != rank)
-        def _():
-            to(place(order)).wait_send()
-
-        return carry
-
-    lax.fori_loop(0, peers, finish, 0)
-    for f in range(peers):
-        out_ref[f] = done[facet_dir_ref[f]]
+    lax.fori_loop(0, layers + LAG, answer, 0)
+
+    with jax.named_scope("finish"):
+        paced = (half - URGENT_LAYERS) * pol_count
+        for count in range(urgent + 1):
+
+            @pl.when((hurry == count) & (layer < layers - 1))
+            def _():
+                transfers(0, peers - 1 - count, send_sem, layer).wait_send()
+
+        @pl.when(layer == layers - 1)
+        def _():
+            transfers(0, peers - 1 - urgent - paced, send_sem, layer).wait_send()
+
+    with jax.named_scope("order"):
+        for f in range(peers):
+            out_ref[f] = done[facet_dir_ref[f]]
 
 
 def shards(gains, visibilities, first_station, second_station, filled_row_count, facet_dir):
     bt_count, pol_count = lax.axis_size("bt"), lax.axis_size("pol")
     peers = bt_count * pol_count
     chans = gains.shape[1]
-    any_spec = pl.BlockSpec(memory_space=pl.ANY)
-    smem = pl.BlockSpec(memory_space=pltpu.SMEM)
+    hbm = pl.BlockSpec(memory_space=pltpu.HBM)
     vmem = pl.BlockSpec(memory_space=pltpu.VMEM)
     rows = 8 * chans * GAIN_SLOT_COUNT
+    operands = (
+        facet_dir,
+        first_station.reshape(GAIN_SLOT_COUNT, LANES),
+        second_station.reshape(GAIN_SLOT_COUNT, LANES),
+        gains,
+        visibilities,
+    )
     return pl.pallas_call(
         functools.partial(kernel, peers, bt_count, pol_count),
         name="correct",
         out_shape=jax.ShapeDtypeStruct(visibilities.shape, visibilities.dtype),
-        in_specs=[smem, smem, vmem, vmem, any_spec, any_spec],
+        in_specs=[pl.BlockSpec(memory_space=pltpu.SMEM)] + [hbm] * 5,
         out_specs=vmem,
         scratch_shapes=[
+            pltpu.SMEM(facet_dir.shape, jnp.int32),
+            pltpu.VMEM((GAIN_SLOT_COUNT, LANES), jnp.int32),
+            pltpu.VMEM((GAIN_SLOT_COUNT, LANES), jnp.int32),
             pltpu.VMEM(gains.shape[1:], jnp.float32),
             pltpu.VMEM((peers, TILES, 8, LANES), jnp.float32),
             pltpu.VMEM((peers, TILES, 8, LANES), jnp.float32),
@@ -242,20 +410,15 @@
             pltpu.VMEM((rows, LANES), jnp.float32),
             pltpu.VMEM((rows, LANES), jnp.float32),
             pltpu.VMEM((rows, LANES), jnp.float32),
+            pltpu.SemaphoreType.DMA((5,)),
+            pltpu.SemaphoreType.DMA((URGENT_LAYERS * pol_count,)),
             pltpu.SemaphoreType.DMA,
-            pltpu.SemaphoreType.DMA,
-            pltpu.SemaphoreType.DMA((peers,)),
-            pltpu.SemaphoreType.DMA((peers,)),
+            pltpu.SemaphoreType.DMA((bt_count,)),
+            pltpu.SemaphoreType.REGULAR((bt_count,)),
+            pltpu.SemaphoreType.REGULAR,
         ],
-        compiler_params=pltpu.CompilerParams(collective_id=0, has_side_effects=True),
-    )(
-        filled_row_count,
-        facet_dir,
-        first_station.reshape(GAIN_SLOT_COUNT, LANES),
-        second_station.reshape(GAIN_SLOT_COUNT, LANES),
-        gains,
-        visibilities,
-    )
+        compiler_params=pltpu.CompilerParams(collective_id=0, has_side_effects=True, vmem_limit_bytes=8 << 20),
+    )(filled_row_count, *(pltpu.with_memory_space_constraint(x, pltpu.HBM) for x in operands))
 
 
 def solution(mesh):

time: 85.5 us -> 57.6 us (0.67)
  the two profiles are of different devices: /device:TPU:64 before, /device:TPU:345 now
where the time goes in v2:
time: 57.6 us; the launch traced here: 57.5 us
  Pallas kernels  56 us (97%)
  local copies, waits for them, and re-layouts  0.8 us (1%)
  between operations  0.66 us (1%)
    pallas_call x1, Pallas kernels, shards(): pl.pallas_call(functools.partial(kernel, peers, bt_count, pol_count), nam...  56 us

profile of v2, /device:TPU:345, one launch (start us, length us, event | category | flops | bytes accessed | tf_op | source)
XLA Modules:
  0.0 57.5 jit_solution(5915692689651583050)
XLA Ops:
  0.7 56.0 %correct.1 = bf16[32,2,8,512]{3,2,1,0:T(8,128)(2,1)S(1)} custom-call(s32[1]{0:T(128)S(6)} %copy.8.filled_ref, s32[32]{0:T(128)} %facet_dir_hbm.1, s32[4,128]{1,0:T(4,128)} %bitcast.2, s32[4,128]{1,0:T(4,128)} %bitcast.3, f32[1,2,8,7936]{3,2,1,0:T(8,128)} %gains_hbm.1, bf16[32,2,8,512]{3,2,1,0:T(8,128)(2,1)} %vis_hbm.1), custom_call_target="tpu_custom_call" | custom-call | tf_op jit(solution)/shard_map/correct/pallas_call | solution.py:394
  56.7 0.8 %copy.9 = bf16[32,2,8,512]{3,2,1,0:T(8,128)(2,1)} copy(bf16[32,2,8,512]{3,2,1,0:T(8,128)(2,1)S(1)} %correct.1) | data formatting | bytes 1048576

commit v3 on v2

--- a/solution.py
+++ b/solution.py
@@ -12,9 +12,11 @@
 LANES = 128
 TILES = 5
 IN_FLIGHT = 2
-URGENT_LAYERS = 2
-LATE_LAYERS = 3
+FREE_LAYERS = 3
 LAG = 4
+LAST_GO = 4
+LOOK_AHEAD = 1
+EARLY = 4
 MESH = pl.DeviceIdType.MESH
 
 
@@ -67,13 +69,17 @@
     chans = held.shape[0]
     slots = GAIN_SLOT_COUNT
     layers, half = peers // pol_count, bt_count // 2
-    rotate = jnp.where((lax.axis_index("obs") == 0) & (lax.axis_index("freq") == 0), 1, 0)
-    rank = lax.rem(lax.axis_index("bt") * pol_count + lax.axis_index("pol") + peers - rotate, peers)
+    own_place = lax.axis_index("bt") * pol_count + lax.axis_index("pol")
+    behind = (layers - 2) * pol_count - 1
+    shifted = (lax.axis_index("obs") == 0) & (lax.axis_index("freq") == 0)
+    rank = jnp.where(own_place == 0, behind, jnp.where(own_place <= behind, own_place - 1, own_place))
+    rank = jnp.where(shifted, rank, own_place)
     layer = rank // pol_count
     partner = layer * pol_count + lax.rem(rank + 1, pol_count)
 
     def place(order):
-        return lax.rem(order + rotate, peers)
+        moved = jnp.where(order == behind, 0, jnp.where(order < behind, order + 1, order))
+        return jnp.where(shifted, moved, order)
 
     def device(order):
         where = place(order)
@@ -138,7 +144,7 @@
         loads[0].wait()
     lane = lax.broadcasted_iota(jnp.int32, (8, LANES), 1)
     total_slots = peers * slots
-    urgent = URGENT_LAYERS * pol_count
+    urgent = FREE_LAYERS * pol_count
 
     def pack(where):
         base = where * slots
@@ -166,59 +172,124 @@
         to(order, urgent_sem.at[order]).wait_send()
         return carry
 
-    hurry = jnp.minimum(rank, urgent)
-    for where in range(urgent + 1):
+    free = jnp.clip((layers - layer + 2) // 2, 1, FREE_LAYERS)
+    hurry = jnp.minimum(rank, free * pol_count)
+    for where in range(IN_FLIGHT + 1):
         pack(where)
     with jax.named_scope("urgent"):
         lax.fori_loop(0, jnp.minimum(rank, IN_FLIGHT), hasten, 0)
-        for where in range(urgent + 1, peers):
+        for where in range(IN_FLIGHT + 1, peers):
             pack(where)
         lax.fori_loop(IN_FLIGHT, hurry, hasten_next, 0)
         lax.fori_loop(jnp.maximum(hurry - IN_FLIGHT, 0), hurry, hastened, 0)
 
-    late = layers - LATE_LAYERS
-    far_above = jnp.where(rank < urgent, layers, jnp.minimum(jnp.maximum(layer + half, late), layers))
-    far_below = jnp.where(layer < late, URGENT_LAYERS, jnp.maximum(layer - half + 1, URGENT_LAYERS))
+    gated = layers - FREE_LAYERS - 1
+
+    def far_from(low):
+        return jnp.maximum(low + half + 1, jnp.where(low == 0, layers, jnp.maximum(layers + 1 - 2 * low, gated)))
+
+    above_from = jnp.where(layer < FREE_LAYERS, far_from(layer), jnp.minimum(far_from(layer), gated + 1))
+    above_from = jnp.where(layer <= 1, layers, jnp.minimum(jnp.maximum(above_from, layer + 1), layers))
+    alone = shifted & (rank == behind)
+    far_below = jnp.where((layer < gated) | alone, free, jnp.maximum(layer - half, free))
+
+    def drain():
+        paced = jnp.where(layer == layers - 1, (far_below - free) * pol_count, 0)
+        paced = jnp.where((layer > 0) & (layer < half), (layers - above_from) * pol_count, paced)
+        for count in range(1, peers):
+
+            @pl.when(peers - 1 - hurry - paced == count)
+            def _():
+                transfers(0, count, send_sem, layer).wait_send()
+
+    def wait_turn():
+        with jax.named_scope("go"):
+            pl.semaphore_wait(go, 1)
 
     def send_far():
-        @pl.when((rank >= urgent) & (layer < half))
-        def _():
-            with jax.named_scope("go"):
-                pl.semaphore_wait(go, 1)
-            lax.fori_loop(far_above * pol_count, peers, send, 0)
-
-        @pl.when((layer >= late) & (layer < layers - 1))
+        @pl.when((layer >= gated) & (layer < layers - 1))
         def _():
             def turn_of(low, carry):
-                with jax.named_scope("go"):
-                    pl.semaphore_wait(go, 1)
+                wait_turn()
                 for core in range(pol_count):
                     send(low * pol_count + core, 0)
                 return carry
 
-            lax.fori_loop(URGENT_LAYERS, far_below, turn_of, 0)
+            lax.fori_loop(free, far_below, turn_of, 0)
 
         @pl.when(layer == layers - 1)
         def _():
-            def turn_of(low, carry):
+            def release(low):
                 @pl.when(rank == peers - pol_count)
                 def _():
-                    for core in range(pol_count):
-                        signal(go, low * pol_count + core)
-
-                    def release(order, carry):
+                    def allow(order, carry):
                         signal(go, order)
                         return carry
 
-                    lax.fori_loop(jnp.maximum(low + half, late) * pol_count, peers - pol_count, release, 0)
-
+                    def allow_gated(order, carry):
+                        @pl.when(jnp.logical_not(shifted & (order == behind)))
+                        def _():
+                            signal(go, order)
+
+                        return carry
+
+                    lax.fori_loop(far_from(low) * pol_count, peers - pol_count, allow_gated, 0)
+
+                    @pl.when(low == LAST_GO)
+                    def _():
+                        lax.fori_loop(half * pol_count, peers - pol_count, allow, 0)
+
+            for low in range(1, 1 + LOOK_AHEAD):
+                release(low)
+
+            def turn_of(low, carry):
+                release(low + LOOK_AHEAD)
                 for core in range(pol_count):
                     to(low * pol_count + core, urgent_sem.at[core]).start()
                 for core in range(pol_count):
                     to(low * pol_count + core, urgent_sem.at[core]).wait_send()
                 return carry
 
-            lax.fori_loop(URGENT_LAYERS, far_below, turn_of, 0)
+            lax.fori_loop(free, far_below, turn_of, 0)
+
+    def answer_last():
+        @pl.when((layer >= half) & (layer < layers - 1))
+        def _():
+            wait_turn()
+            lax.fori_loop(above_from * pol_count, peers, send, 0)
+
+        @pl.when((layer > 0) & (layer < half))
+        def _():
+            base = above_from * pol_count
+
+            @pl.when(layer == 1)
+            def _():
+                drain()
+
+            @pl.when(layer > 1)
+            def _():
+                wait_turn()
+
+                def start(order, carry):
+                    to(order, urgent_sem.at[order - base]).start()
+                    return carry
+
+                lax.fori_loop(base, peers, start, 0)
+
+                @pl.when((layer < half - 1) & (layer >= EARLY))
+                def _():
+                    signal(go, rank + pol_count)
+
+                def wait(order, carry):
+                    to(order, urgent_sem.at[order - base]).wait_send()
+                    return carry
+
+                with jax.named_scope("left"):
+                    lax.fori_loop(base, peers, wait, 0)
+
+            @pl.when((layer < half - 1) & (layer < EARLY))
+            def _():
+                signal(go, rank + pol_count)
 
     incoming[rank] = outgoing[place(rank)]
     with jax.named_scope("loads"):
@@ -296,10 +367,11 @@
                 data_rows[at : at + 8, :] = vis[facet, chan, :, slot * LANES : (slot + 1) * LANES].astype(jnp.float32)
         correct(order, where)
 
-    with jax.named_scope("own"):
-        take(rank)
     above = layers - 1 - layer
-    near_above = far_above - 1 - layer
+    near_above = above_from - 1 - layer
+
+    last_step = jnp.where(layer <= 1, layers - 3, near_above + 1 + jnp.where(layer < half, layer, 0))
+    last_turn = jnp.maximum(above, jnp.minimum(last_step, layers - 1) + LAG)
 
     def answer(turn, carry):
         @pl.when((turn == 0) & (rank < partner))
@@ -307,7 +379,7 @@
             pl.semaphore_wait(entered.at[layer], pol_count - 1)
             send(partner, 0)
 
-        @pl.when((turn == 0) & (rank > partner) & (rank >= urgent))
+        @pl.when((turn == 0) & (rank > partner) & (layer >= free))
         def _():
             send(partner, 0)
 
@@ -316,7 +388,7 @@
             with jax.named_scope("hello"):
                 pl.semaphore_wait(entered.at[layer + turn], pol_count)
 
-            @pl.when(layer + turn < far_above)
+            @pl.when(layer + turn < above_from)
             def _():
                 for core in range(pol_count):
                     send((layer + turn) * pol_count + core, 0)
@@ -329,16 +401,27 @@
                 send(low * pol_count + core, 0)
             return carry
 
-        lax.fori_loop(first, last, send_near, 0)
+        @pl.when(layer < layers - 1)
+        def _():
+            lax.fori_loop(first, last, send_near, 0)
 
         @pl.when(turn == above)
         def _():
             send_far()
 
+        @pl.when(layer == layers - 1)
+        def _():
+            lax.fori_loop(first, last, send_near, 0)
+
         step = turn - LAG
 
+        @pl.when(turn == last_turn)
+        def _():
+            answer_last()
+
         @pl.when(step == 0)
         def _():
+            take(rank)
             transfers(partner, pol_count - 1, send_sem, layer).wait_recv()
             take(partner)
 
@@ -361,16 +444,10 @@
     lax.fori_loop(0, layers + LAG, answer, 0)
 
     with jax.named_scope("finish"):
-        paced = (half - URGENT_LAYERS) * pol_count
-        for count in range(urgent + 1):
-
-            @pl.when((hurry == count) & (layer < layers - 1))
-            def _():
-                transfers(0, peers - 1 - count, send_sem, layer).wait_send()
-
-        @pl.when(layer == layers - 1)
-        def _():
-            transfers(0, peers - 1 - urgent - paced, send_sem, layer).wait_send()
+
+        @pl.when(layer != 1)
+        def _():
+            drain()
 
     with jax.named_scope("order"):
         for f in range(peers):
@@ -411,7 +488,7 @@
             pltpu.VMEM((rows, LANES), jnp.float32),
             pltpu.VMEM((rows, LANES), jnp.float32),
             pltpu.SemaphoreType.DMA((5,)),
-            pltpu.SemaphoreType.DMA((URGENT_LAYERS * pol_count,)),
+            pltpu.SemaphoreType.DMA(((FREE_LAYERS + 1) * pol_count,)),
             pltpu.SemaphoreType.DMA,
             pltpu.SemaphoreType.DMA((bt_count,)),
             pltpu.SemaphoreType.REGULAR((bt_count,)),

time: 57.6 us -> 57.1 us (level)
  the two profiles are of different devices: /device:TPU:345 before, /device:TPU:579 now
where the time goes in v3:
time: 57.1 us; the launch traced here: 57 us
  Pallas kernels  55.5 us (97%)
  local copies, waits for them, and re-layouts  0.8 us (1%)
  between operations  0.66 us (1%)
    pallas_call x1, Pallas kernels, shards(): pl.pallas_call(functools.partial(kernel, peers, bt_count, pol_count), nam...  55.5 us

profile of v3, /device:TPU:579, one launch (start us, length us, event | category | flops | bytes accessed | tf_op | source)
XLA Modules:
  0.0 57.0 jit_solution(5210452804623816661)
XLA Ops:
  0.7 55.5 %correct.1 = bf16[32,2,8,512]{3,2,1,0:T(8,128)(2,1)S(1)} custom-call(s32[1]{0:T(128)S(6)} %copy.8.filled_ref, s32[32]{0:T(128)} %facet_dir_hbm.1, s32[4,128]{1,0:T(4,128)} %bitcast.2, s32[4,128]{1,0:T(4,128)} %bitcast.3, f32[1,2,8,7936]{3,2,1,0:T(8,128)} %gains_hbm.1, bf16[32,2,8,512]{3,2,1,0:T(8,128)(2,1)} %vis_hbm.1), custom_call_target="tpu_custom_call" | custom-call | tf_op jit(solution)/shard_map/correct/pallas_call | solution.py:471
  56.2 0.8 %copy.9 = bf16[32,2,8,512]{3,2,1,0:T(8,128)(2,1)} copy(bf16[32,2,8,512]{3,2,1,0:T(8,128)(2,1)S(1)} %correct.1) | data formatting | bytes 1048576

commit v4 on v3

--- a/solution.py
+++ b/solution.py
@@ -14,9 +14,9 @@
 IN_FLIGHT = 2
 FREE_LAYERS = 3
 LAG = 4
-LAST_GO = 4
+LAST_GO = 6
 LOOK_AHEAD = 1
-EARLY = 4
+EARLY = 5
 MESH = pl.DeviceIdType.MESH
 
 
@@ -172,7 +172,7 @@
         to(order, urgent_sem.at[order]).wait_send()
         return carry
 
-    free = jnp.clip((layers - layer + 2) // 2, 1, FREE_LAYERS)
+    free = jnp.clip(layers - layer, 1, FREE_LAYERS)
     hurry = jnp.minimum(rank, free * pol_count)
     for where in range(IN_FLIGHT + 1):
         pack(where)
@@ -186,7 +186,7 @@
     gated = layers - FREE_LAYERS - 1
 
     def far_from(low):
-        return jnp.maximum(low + half + 1, jnp.where(low == 0, layers, jnp.maximum(layers + 1 - 2 * low, gated)))
+        return jnp.maximum(low + half + 1, jnp.where(low == 0, layers, jnp.where(low < FREE_LAYERS, layers - low, gated)))
 
     above_from = jnp.where(layer < FREE_LAYERS, far_from(layer), jnp.minimum(far_from(layer), gated + 1))
     above_from = jnp.where(layer <= 1, layers, jnp.minimum(jnp.maximum(above_from, layer + 1), layers))
@@ -252,6 +252,16 @@
 
             lax.fori_loop(free, far_below, turn_of, 0)
 
+    def answers_left():
+        base = above_from * pol_count
+
+        def wait(order, carry):
+            to(order, urgent_sem.at[order - base]).wait_send()
+            return carry
+
+        with jax.named_scope("left"):
+            lax.fori_loop(base, peers, wait, 0)
+
     def answer_last():
         @pl.when((layer >= half) & (layer < layers - 1))
         def _():
@@ -280,12 +290,9 @@
                 def _():
                     signal(go, rank + pol_count)
 
-                def wait(order, carry):
-                    to(order, urgent_sem.at[order - base]).wait_send()
-                    return carry
-
-                with jax.named_scope("left"):
-                    lax.fori_loop(base, peers, wait, 0)
+                @pl.when(layer < EARLY)
+                def _():
+                    answers_left()
 
             @pl.when((layer < half - 1) & (layer < EARLY))
             def _():
@@ -444,6 +451,10 @@
     lax.fori_loop(0, layers + LAG, answer, 0)
 
     with jax.named_scope("finish"):
+
+        @pl.when((layer >= EARLY) & (layer < half))
+        def _():
+            answers_left()
 
         @pl.when(layer != 1)
         def _():

time: 57.1 us -> 56 us (0.981)
  the two profiles are of different devices: /device:TPU:579 before, /device:TPU:479 now
where the time goes in v4:
time: 56 us; the launch traced here: 55.9 us
  Pallas kernels  54.4 us (97%)
  local copies, waits for them, and re-layouts  0.8 us (1%)
  between operations  0.66 us (1%)
    pallas_call x1, Pallas kernels, shards(): pl.pallas_call(functools.partial(kernel, peers, bt_count, pol_count), nam...  54.4 us

profile of v4, /device:TPU:479, one launch (start us, length us, event | category | flops | bytes accessed | tf_op | source)
XLA Modules:
  0.0 55.9 jit_solution(13358907290505450404)
XLA Ops:
  0.7 54.4 %correct.1 = bf16[32,2,8,512]{3,2,1,0:T(8,128)(2,1)S(1)} custom-call(s32[1]{0:T(128)S(6)} %copy.8.filled_ref, s32[32]{0:T(128)} %facet_dir_hbm.1, s32[4,128]{1,0:T(4,128)} %bitcast.2, s32[4,128]{1,0:T(4,128)} %bitcast.3, f32[1,2,8,7936]{3,2,1,0:T(8,128)} %gains_hbm.1, bf16[32,2,8,512]{3,2,1,0:T(8,128)(2,1)} %vis_hbm.1), custom_call_target="tpu_custom_call" | custom-call | tf_op jit(solution)/shard_map/correct/pallas_call | solution.py:482
  55.1 0.8 %copy.9 = bf16[32,2,8,512]{3,2,1,0:T(8,128)(2,1)} copy(bf16[32,2,8,512]{3,2,1,0:T(8,128)(2,1)S(1)} %correct.1) | data formatting | bytes 1048576

commit v5 on v4

--- a/solution.py
+++ b/solution.py
@@ -11,7 +11,7 @@
 GAIN_SLOT_COUNT = 4
 LANES = 128
 TILES = 5
-IN_FLIGHT = 2
+IN_FLIGHT = 3
 FREE_LAYERS = 3
 LAG = 4
 LAST_GO = 6
@@ -177,7 +177,7 @@
     for where in range(IN_FLIGHT + 1):
         pack(where)
     with jax.named_scope("urgent"):
-        lax.fori_loop(0, jnp.minimum(rank, IN_FLIGHT), hasten, 0)
+        lax.fori_loop(0, jnp.minimum(hurry, IN_FLIGHT), hasten, 0)
         for where in range(IN_FLIGHT + 1, peers):
             pack(where)
         lax.fori_loop(IN_FLIGHT, hurry, hasten_next, 0)

time: 56 us -> 55.8 us (level)
  no operation moved by 1% of the time
where the time goes in v5:
time: 55.8 us; the launch traced here: 55.7 us
  Pallas kernels  54.2 us (97%)
  local copies, waits for them, and re-layouts  0.8 us (1%)
  between operations  0.66 us (1%)
    pallas_call x1, Pallas kernels, shards(): pl.pallas_call(functools.partial(kernel, peers, bt_count, pol_count), nam...  54.2 us

profile of v5, /device:TPU:479, one launch (start us, length us, event | category | flops | bytes accessed | tf_op | source)
XLA Modules:
  0.0 55.7 jit_solution(11965398315897642590)
XLA Ops:
  0.7 54.2 %correct.1 = bf16[32,2,8,512]{3,2,1,0:T(8,128)(2,1)S(1)} custom-call(s32[1]{0:T(128)S(6)} %copy.8.filled_ref, s32[32]{0:T(128)} %facet_dir_hbm.1, s32[4,128]{1,0:T(4,128)} %bitcast.2, s32[4,128]{1,0:T(4,128)} %bitcast.3, f32[1,2,8,7936]{3,2,1,0:T(8,128)} %gains_hbm.1, bf16[32,2,8,512]{3,2,1,0:T(8,128)(2,1)} %vis_hbm.1), custom_call_target="tpu_custom_call" | custom-call | tf_op jit(solution)/shard_map/correct/pallas_call | solution.py:482
  54.9 0.8 %copy.9 = bf16[32,2,8,512]{3,2,1,0:T(8,128)(2,1)} copy(bf16[32,2,8,512]{3,2,1,0:T(8,128)(2,1)S(1)} %correct.1) | data formatting | bytes 1048576
